TPU v7x, 32 devices: a whole 2x2x4 slice. The times are simulated.
32 devices in a mesh: slab: 8 (over z, y), md: 4 (over x, core).
Axes of the slice: x: 2, y: 2, z: 4, core: 2. Of those that a mesh axis runs over, the one named last changes fastest.
Arguments:
- populations: float32 [19, 16, 256, 128], P(None, 'slab', 'md'), may hold values from 0.02 to 0.1
- relax: float32 [16, 256, 128], P('slab', 'md'), may hold values from 0.8 to 1.8
- owners: int32 [16, 256, 2], P('slab', 'md'), may hold values from 0 to 31, all different within a row; in each aligned block of 64 rows (0 to 63, 64 to 127, ..., all dimensions but the last counted through in order) at most 8 rows name the same one
- positions: float32 [3, 32768], P(None, ('slab', 'md')), may hold values from 0 to 3
- velocities: float32 [3, 32768], P(None, ('slab', 'md')), may hold values from -5 to 5
- neighbours: int32 [32768, 64], P(('slab', 'md')), may hold values from 0 to 1023
- atom_slots: int32 [32768], P(('slab', 'md')), may hold values from 0 to 511
Outputs:
- populations_out: float32 [19, 16, 256, 128], P(None, 'slab', 'md')
- positions_out: float32 [3, 32768], P(None, ('slab', 'md'))
- velocities_out: float32 [3, 32768], P(None, ('slab', 'md'))
- cell_moments: float32 [4, 16, 256], P(None, 'slab', 'md')
Inputs may be any that keep to these rules, and one draw needn't show every extreme that they name: The 64 entries of one z position on one device name any owner at most 8 times in each column k and across k; the 2 owners of one cell differ. `neighbours`: entries index atoms of the same subdomain's block of 1024 atoms; an atom that lists itself is padding.
All inputs are finite; a program needn't handle non-finite values.
Results may differ from a plain program's by a relative error of at most 0.0003.
Values sent between devices are 32-bit elements; how exact they have to be, the bound alone decides.
A program may use at most 64 MiB of HBM per device.

v0:
```python
import functools

import jax
import jax.numpy as jnp
from jax import lax
from jax.experimental import pallas as pl
from jax.experimental.pallas import tpu as pltpu
from jax.sharding import PartitionSpec as P

LB_STEPS = 4
MD_STEPS = 5

ORDER = [13, 1, 7, 9, 11, 5, 15, 18, 14, 2, 8, 10, 12, 6, 16, 17, 0, 3, 4]
lattice_dirs = [
    (0, 0, 0),
    (1, 0, 0),
    (-1, 0, 0),
    (0, 1, 0),
    (0, -1, 0),
    (0, 0, 1),
    (0, 0, -1),
    (1, 1, 0),
    (-1, -1, 0),
    (1, -1, 0),
    (-1, 1, 0),
    (1, 0, 1),
    (-1, 0, -1),
    (1, 0, -1),
    (-1, 0, 1),
    (0, 1, 1),
    (0, -1, -1),
    (0, 1, -1),
    (0, -1, 1),
]
DIRS = [lattice_dirs[i] for i in ORDER]
velocity_scale = 10.0
pair_strength = 0.5
friction = 2.0
time_step = 0.1
highest = lax.Precision.HIGHEST
MESH = pl.DeviceIdType.MESH


def total_of(terms):
    terms = list(terms)
    while len(terms) > 1:
        terms = [a + b for a, b in zip(terms[::2], terms[1::2])] + (
            [terms[-1]] if len(terms) % 2 else []
        )
    return terms[0]


def fields(f):
    density = total_of(f)
    inverse = 1.0 / density
    vel = []
    for axis in range(3):
        plus = total_of(f[p] for p in range(19) if DIRS[p][axis] == 1)
        minus = total_of(f[p] for p in range(19) if DIRS[p][axis] == -1)
        vel.append((plus - minus) * inverse)
    return density, vel


def collided(f, relax):
    density, (vx, vy, vz) = fields(f)
    base = 1.0 - 1.5 * (vx * vx + vy * vy + vz * vz)
    keep = 1.0 - relax
    scale = relax * density
    result = [None] * 19
    for p, c in enumerate(DIRS):
        if result[p] is not None:
            continue
        size = sum(abs(e) for e in c)
        if size == 0:
            result[p] = keep * f[p] + (scale * (1.0 / 3.0)) * base
            continue
        along = total_of(v if e == 1 else -v for e, v in zip(c, (vx, vy, vz)) if e)
        weight = scale * (1.0 / 18.0 if size == 1 else 1.0 / 36.0)
        even = weight * (base + 4.5 * (along * along))
        odd = weight * (3.0 * along)
        q = DIRS.index(tuple(-e for e in c))
        result[p] = keep * f[p] + (even + odd)
        result[q] = keep * f[q] + (even - odd)
    return result


def lattice_kernel(
    n_slab, n_md, f_ref, relax_ref, out_ref, tgt_ref, post, rows_out, rows_in, mean_ref, send, recv
):
    cz, cx, ny = relax_ref.shape
    slab, md = lax.axis_index("slab"), lax.axis_index("md")
    above, below = lax.rem(slab + 1, n_slab), lax.rem(slab + n_slab - 1, n_slab)
    right, left = lax.rem(md + 1, n_md), lax.rem(md + n_md - 1, n_md)
    barrier = pltpu.get_barrier_semaphore()
    peers = [
        (above, md),
        (below, md),
        (slab, right),
        (slab, left),
        (above, right),
        (below, right),
        (above, left),
        (below, left),
    ]
    for peer in peers:
        pl.semaphore_signal(barrier, inc=1, device_id=peer, device_id_type=MESH)

    def load(step, z, x0):
        if step == 0:
            return [f_ref[ORDER[p], z, pl.ds(x0, 8), :] for p in range(19)]
        return [
            post[step - 1, p, z + 1 - c[2], pl.ds(x0 + (8 - c[0]), 8), :]
            for p, c in enumerate(DIRS)
        ]

    def plane(step, z):
        def block(b, carry):
            x0 = pl.multiple_of(b * 8, 8)
            done = collided(load(step, z, x0), relax_ref[z, pl.ds(x0, 8), :])
            for p, c in enumerate(DIRS):
                value = done[p] if c[1] == 0 else pltpu.roll(done[p], c[1] % ny, axis=1)
                post[step, p, z + 1, pl.ds(x0 + 8, 8), :] = value
            return carry

        lax.fori_loop(0, cx // 8, block, 0, unroll=2)

    copies = []
    for step in range(LB_STEPS):

        def copy(slot, src, dst, peer):
            made = pltpu.make_async_remote_copy(
                src_ref=src,
                dst_ref=dst,
                send_sem=send.at[step, slot],
                recv_sem=recv.at[step, slot],
                device_id=peer,
                device_id_type=MESH,
            )
            made.start()
            copies.append(made)
            return made

        now = []
        own = pl.ds(8, cx)
        plane(step, cz - 1)
        if step == 0:
            pl.semaphore_wait(barrier, len(peers))
        now.append(
            copy(
                0,
                post.at[step, pl.ds(4, 5), cz, own, :],
                post.at[step, pl.ds(4, 5), 0, own, :],
                (above, md),
            )
        )
        for z in range(cz - 1):
            plane(step, z)
        for slot, first, count in ((1, 12, 4), (2, 0, 1)):
            now.append(
                copy(
                    slot,
                    post.at[step, pl.ds(first, count), 1, own, :],
                    post.at[step, pl.ds(first, count), cz + 1, own, :],
                    (below, md),
                )
            )
        for side, first, row in ((0, 0, 7 + cx), (1, 8, 8)):
            for j in range(5):
                for z in range(cz):
                    rows_out[step, side, j * cz + z, :] = post[step, first + j, z + 1, row, :]
        for k, (p, z, row) in enumerate(
            ((4, cz, 7 + cx), (0, 1, 7 + cx), (8, cz, 8), (12, 1, 8))
        ):
            rows_out[step, 2 + k, 0, :] = post[step, p, z, row, :]
        for k in range(6):
            height = rows_out.shape[2] if k < 2 else 8
            now.append(
                copy(
                    3 + k,
                    rows_out.at[step, k, pl.ds(0, height), :],
                    rows_in.at[step, k, pl.ds(0, height), :],
                    peers[2 + k],
                )
            )
        for made in now:
            made.wait_recv()
        for side, first, row in ((0, 0, 7), (1, 8, 8 + cx)):
            for j in range(5):
                for z in range(cz):
                    post[step, first + j, z + 1, row, :] = rows_in[step, side, j * cz + z, :]
        for k, (p, z, row) in enumerate(
            ((4, 0, 7), (0, cz + 1, 7), (8, 0, 8 + cx), (12, cz + 1, 8 + cx))
        ):
            post[step, p, z, row, :] = rows_in[step, 2 + k, 0, :]

    for z in range(cz):

        def last(b, carry, z=z):
            x0 = pl.multiple_of(b * 8, 8)
            f = load(LB_STEPS, z, x0)
            for p in range(19):
                out_ref[ORDER[p], z, pl.ds(x0, 8), :] = f[p]
            density, vel = fields(f)
            for c, value in enumerate((*vel, density)):
                mean_ref[c, pl.ds(x0 + z * cx, 8), :] = value
            return carry

        lax.fori_loop(0, cx // 8, last, 0, unroll=2)
    for c in range(4):
        scale = (velocity_scale if c < 3 else 1.0) / ny
        tgt_ref[pl.ds(c, 1), :] = jnp.sum(mean_ref[c].T, axis=0, keepdims=True) * scale
    for made in copies:
        made.wait_send()


def lattice(populations, relax, n_slab, n_md):
    cz, cx, ny = relax.shape
    rows = -(-5 * cz // 8) * 8
    vmem = pl.BlockSpec(memory_space=pltpu.VMEM)
    return pl.pallas_call(
        functools.partial(lattice_kernel, n_slab, n_md),
        out_shape=(
            jax.ShapeDtypeStruct(populations.shape, jnp.float32),
            jax.ShapeDtypeStruct((4, cz * cx), jnp.float32),
        ),
        in_specs=[vmem, vmem],
        out_specs=(vmem, vmem),
        scratch_shapes=[
            pltpu.VMEM((LB_STEPS, 19, cz + 2, cx + 16, ny), jnp.float32),
            pltpu.VMEM((LB_STEPS, 6, rows, ny), jnp.float32),
            pltpu.VMEM((LB_STEPS, 6, rows, ny), jnp.float32),
            pltpu.VMEM((4, cz * cx, ny), jnp.float32),
            pltpu.SemaphoreType.DMA((LB_STEPS, 9)),
            pltpu.SemaphoreType.DMA((LB_STEPS, 9)),
        ],
        compiler_params=pltpu.CompilerParams(
            collective_id=0, has_side_effects=True, vmem_limit_bytes=32 * 1024 * 1024
        ),
        name="lattice",
    )(populations, relax)


def lane_gather(table, index):
    return jnp.take_along_axis(table, index, axis=1, mode="promise_in_bounds")


def particle_kernel(
    pos_ref, vel_ref, nbr_ref, slots_ref, recv_ref, pos_out, vel_out, mom_ref, lists, at, pull, data, hits
):
    atoms, entries = nbr_ref.shape
    groups = atoms // 128
    slot_count = recv_ref.shape[1]
    for g in range(groups):
        here = pl.ds(g * 128, 128)
        lists[g] = nbr_ref[here, :].T
        for c in range(3):
            at[c, pl.ds(g, 1), :] = pos_ref[pl.ds(c, 1), here]
            at[3 + c, pl.ds(g, 1), :] = vel_ref[pl.ds(c, 1), here]
        label = lax.broadcasted_iota(jnp.int32, (slot_count, 128), 0)
        same = label == slots_ref[pl.ds(g, 1), :]
        hits[:, here] = jnp.where(same, 1.0, 0.0).astype(jnp.bfloat16)
    slots = slots_ref[...]
    lane, row = slots & 127, slots >> 7
    goal = []
    for c in range(4):
        value = jnp.zeros((groups, 128), jnp.float32)
        for h in range(slot_count // 128):
            table = jnp.broadcast_to(recv_ref[pl.ds(c, 1), pl.ds(h * 128, 128)], (groups, 128))
            value = jnp.where(row == h, lane_gather(table, lane), value)
        goal.append(value)
    rate = friction * goal[3]

    def one_step(step, carry):
        def one_group(g, inner):
            own = [jnp.broadcast_to(at[c, pl.ds(g, 1), :], (8, 128)) for c in range(3)]
            sums = [jnp.zeros((8, 128), jnp.float32)] * 3
            for k in range(0, entries, 8):
                index = lists[g, pl.ds(k, 8), :]
                lane, row = index & 127, index >> 7
                found = [None] * 3
                for h in range(groups):
                    pick = row == h
                    for c in range(3):
                        table = jnp.broadcast_to(at[c, pl.ds(h, 1), :], (8, 128))
                        value = lane_gather(table, lane)
                        found[c] = value if h == 0 else jnp.where(pick, value, found[c])
                gap = [found[c] - own[c] for c in range(3)]
                weight = jnp.exp(-0.5 * (gap[0] * gap[0] + gap[1] * gap[1] + gap[2] * gap[2]))
                sums = [sums[c] + gap[c] * weight for c in range(3)]
            for c in range(3):
                pull[c, pl.ds(g, 1), :] = jnp.sum(sums[c], axis=0, keepdims=True)
            return inner

        lax.fori_loop(0, groups, one_group, 0)
        for c in range(3):
            vel = at[3 + c]
            force = pair_strength * pull[c] + rate * (goal[c] - vel)
            vel = vel + time_step * force
            at[3 + c] = vel
            at[c] = at[c] + time_step * vel
        return carry

    lax.fori_loop(0, MD_STEPS, one_step, 0)
    at[6] = at[3] * at[3] + at[4] * at[4] + at[5] * at[5]
    data[...] = jnp.ones(data.shape, jnp.float32)
    for c in range(4):
        rest = at[3 + c]
        for part in range(3):
            piece = rest.astype(jnp.bfloat16).astype(jnp.float32)
            rest = rest - piece
            for g in range(groups):
                data[pl.ds(part * 4 + c, 1), pl.ds(g * 128, 128)] = piece[g : g + 1, :]
    for g in range(groups):
        here = pl.ds(g * 128, 128)
        for c in range(3):
            pos_out[pl.ds(c, 1), here] = at[c, pl.ds(g, 1), :]
            vel_out[pl.ds(c, 1), here] = at[3 + c, pl.ds(g, 1), :]
    sums = lax.dot_general(
        data[...].astype(jnp.bfloat16),
        hits[...],
        (((1,), (1,)), ((), ())),
        preferred_element_type=jnp.float32,
    )
    mom_ref[...] = (sums[0:4] + sums[4:8] + sums[8:12]) / jnp.maximum(sums[12:13], 1.0)


def particles(pos, vel, nbr, slots, recv):
    atoms, entries = nbr.shape
    slot_count = recv.shape[1]
    groups = atoms // 128
    vmem = pl.BlockSpec(memory_space=pltpu.VMEM)
    return pl.pallas_call(
        particle_kernel,
        out_shape=(
            jax.ShapeDtypeStruct(pos.shape, jnp.float32),
            jax.ShapeDtypeStruct(vel.shape, jnp.float32),
            jax.ShapeDtypeStruct((4, slot_count), jnp.float32),
        ),
        in_specs=[vmem] * 5,
        out_specs=(vmem,) * 3,
        scratch_shapes=[
            pltpu.VMEM((groups, entries, 128), jnp.int32),
            pltpu.VMEM((7, groups, 128), jnp.float32),
            pltpu.VMEM((3, groups, 128), jnp.float32),
            pltpu.VMEM((16, atoms), jnp.float32),
            pltpu.VMEM((slot_count, atoms), jnp.bfloat16),
        ],
        name="particles",
    )(pos, vel, nbr, slots.reshape(groups, 128), recv)


def on_device(populations, relax, owners, positions, velocities, neighbours, atom_slots):
    cz_len, cx_len, _ = relax.shape
    n_slab = lax.axis_size("slab")
    n_md = lax.axis_size("md")
    f, targets = lattice(populations, relax, n_slab, n_md)
    top = owners.shape[2]
    devices = n_slab * n_md
    most = max(2, 2 * cx_len * top // devices)
    cap = cz_len * most
    own = owners.reshape(-1)
    onehot = (own[:, None] == jnp.arange(devices, dtype=jnp.int32)[None, :]).astype(jnp.int32)
    rank = jnp.sum((jnp.cumsum(onehot, axis=0) - onehot) * onehot, axis=1)
    dest = own * cap + rank
    placed = (dest[:, None] == jnp.arange(devices * cap, dtype=jnp.int32)[None, :]).astype(
        jnp.float32
    )
    vals = jnp.repeat(targets, top, axis=1)
    outgoing = jnp.dot(vals, placed, precision=highest, preferred_element_type=jnp.float32)
    arrived = lax.all_to_all(
        outgoing.reshape(4, devices, cap), ("slab", "md"), split_axis=1, concat_axis=1, tiled=True
    )
    arrived = arrived.reshape(4, devices * cap)
    pos_out, vel_out, moms = particles(positions, velocities, neighbours, atom_slots, arrived)
    returned = lax.all_to_all(
        moms.reshape(4, devices, cap), ("slab", "md"), split_axis=1, concat_axis=1, tiled=True
    )
    returned = returned.reshape(4, devices * cap)
    picked = jnp.dot(returned, placed.T, precision=highest, preferred_element_type=jnp.float32)
    cell_moments = jnp.sum(picked.reshape(4, cz_len * cx_len, top), axis=2).reshape(
        4, cz_len, cx_len
    )
    return (f, pos_out, vel_out, cell_moments)


def solution(mesh):
    return jax.shard_map(
        on_device,
        mesh=mesh,
        in_specs=(
            P(None, "slab", "md", None),
            P("slab", "md", None),
            P("slab", "md", None),
            P(None, ("slab", "md")),
            P(None, ("slab", "md")),
            P(("slab", "md"), None),
            P(("slab", "md")),
        ),
        out_specs=(
            P(None, "slab", "md", None),
            P(None, ("slab", "md")),
            P(None, ("slab", "md")),
            P(None, "slab", "md"),
        ),
        check_vma=False,
    )
```

profile of v0, /device:TPU:0, one launch (start us, length us, event | category | flops | bytes accessed | tf_op | source)
XLA Modules:
  0.0 94.2 jit_solution(15361500636544598617)
XLA Ops:
  0.6 0.8 copy.35
  1.4 0.1 reshape.102
  1.6 0.1 eq.77
  1.7 0.0 copy-start
  1.7 1.3 %copy-done = f32[19,2,64,128]{3,2,1,0:T(8,128)S(1)} copy-done((f32[19,2,64,128]{3,2,1,0:T(8,128)S(1)}, f32[19,2,64,128]{3,2,1,0:T(8,128)}, u32[]{:S(2)}) %copy-start) | copy-done | bytes 1245208
  3.0 0.0 copy-start.1
  3.0 0.8 copy-done.1
  3.9 0.0 copy-start.2
  3.9 46.4 %lattice.1 = (f32[19,2,64,128]{3,2,1,0:T(8,128)S(1)}, f32[4,128]{1,0:T(4,128)S(1)}) custom-call(f32[19,2,64,128]{3,2,1,0:T(8,128)S(1)} %copy-done, f32[2,64,128]{2,1,0:T(8,128)S(1)} %copy-done.1), custom_call_target="tpu_custom_call" | custom-call | tf_op jit(solution)/shard_map/lattice/pallas_call | solution.py:220
  50.3 0.1 copy.34
  50.4 0.6 reduce-window.6
  51.0 0.2 slice_reduce_fusion
  51.2 0.1 fusion.7
  51.3 0.1 broadcast_compare_fusion
  51.5 0.0 copy-start.3
  51.5 2.4 %fusion.2 = f32[4,32,16]{2,0,1:T(4,128)} fusion(f32[4,256,1]{0,1,2:T(8,128)S(1)} %bitcast.30, pred[32,16,256]{2,0,1:T(32,128)(4,1)S(1)} %broadcast_compare_fusion), kind=kOutput, calls=%fused_computation.3 | convolution fusion | flops 6291456 | bytes 143360 | tf_op jit(solution)/shard_map/dot_general | solution.py:369
  54.0 2.6 %all-to-all-start = ((f32[4,32,16]{2,0,1:T(4,128)}), f32[4,32,16]{2,0,1:T(4,128)S(1)}, u32[]{:S(2)}, u32[]{:S(2)}) async-start(f32[4,32,16]{2,0,1:T(4,128)} %fusion.2), calls=%async_computation | async-start | bytes 131072 | tf_op jit(solution)/shard_map/all_to_all | solution.py:370
  56.5 0.0 copy-done.2
  56.5 1.0 %copy.41.nbr_ref = s32[1024,64]{1,0:T(8,128)} copy(s32[1024,64]{0,1:T(8,128)S(1)} %copy-done.2) | data formatting | bytes 524288 | tf_op args[5]
  57.5 6.4 %all-to-all-done = f32[4,32,16]{2,0,1:T(4,128)S(1)} async-done(((f32[4,32,16]{2,0,1:T(4,128)}), f32[4,32,16]{2,0,1:T(4,128)S(1)}, u32[]{:S(2)}, u32[]{:S(2)}) %all-to-all-start) | async-done | bytes 8224 | tf_op jit(solution)/shard_map/all_to_all | solution.py:370
  63.9 0.7 reshape.104.recv_ref
  64.6 15.9 %particles.1 = (f32[3,1024]{1,0:T(4,128)}, f32[3,1024]{1,0:T(4,128)}, f32[4,512]{1,0:T(4,128)}) custom-call(f32[3,1024]{1,0:T(4,128)} %pos_ref.1, f32[3,1024]{1,0:T(4,128)} %vel_ref.1, s32[1024,64]{1,0:T(8,128)} %copy.41.nbr_ref, s32[8,128]{1,0:T(8,128)} %bitcast.31, f32[4,512]{1,0:T(4,128)} %reshape.104.recv_ref), custom_call_target="tpu_custom_call" | custom-call | tf_op jit(solution)/shard_map/particles/pallas_call | solution.py:332
  80.5 0.8 reshape.105
  81.3 0.7 copy.42
  82.0 2.6 %all-to-all-start.1 = ((f32[4,32,16]{2,0,1:T(4,128)}), f32[4,32,16]{2,0,1:T(4,128)S(1)}, u32[]{:S(2)}, u32[]{:S(2)}) async-start(f32[4,32,16]{2,0,1:T(4,128)} %copy.42), calls=%async_computation.1 | async-start | bytes 131072 | tf_op jit(solution)/shard_map/all_to_all | solution.py:375
  84.5 0.0 copy-done.3
  84.6 0.1 reduce_sum.21
  84.7 0.1 mul.26
  84.8 0.1 copy.45
  84.9 7.1 %all-to-all-done.1 = f32[4,32,16]{2,0,1:T(4,128)S(1)} async-done(((f32[4,32,16]{2,0,1:T(4,128)}), f32[4,32,16]{2,0,1:T(4,128)S(1)}, u32[]{:S(2)}, u32[]{:S(2)}) %all-to-all-start.1) | async-done | bytes 8224 | tf_op jit(solution)/shard_map/all_to_all | solution.py:375
  92.0 0.1 reshape.109
  92.1 0.4 convolution_reduce_fusion
  92.5 0.7 reshape.107
  93.2 1.0 %copy.56 = f32[19,2,64,128]{3,2,1,0:T(8,128)} copy(f32[19,2,64,128]{3,2,1,0:T(8,128)S(1)} %get-tuple-element.18) | data formatting | bytes 2490368
  (11 shorter events, 0.1 us)
Async XLA Ops:
  1.7 1.3 %copy-start = (f32[19,2,64,128]{3,2,1,0:T(8,128)S(1)}, f32[19,2,64,128]{3,2,1,0:T(8,128)}, u32[]{:S(2)}) copy-start(f32[19,2,64,128]{3,2,1,0:T(8,128)} %f_ref.1) | copy-start | bytes 3735556
  3.0 0.8 copy-start.1
  3.9 52.7 %copy-start.2 = (s32[1024,64]{0,1:T(8,128)S(1)}, s32[1024,64]{0,1:T(8,128)}, u32[]{:S(2)}) copy-start(s32[1024,64]{0,1:T(8,128)} %param.12) | copy-start | bytes 786436
  51.5 33.0 %copy-start.3 = (s32[2,64,2]{1,2,0:T(2,128)S(1)}, s32[2,64,2]{1,2,0:T(2,128)}, u32[]{:S(2)}) copy-start(s32[2,64,2]{1,2,0:T(2,128)} %param.9) | copy-start | bytes 3076
  54.0 10.0 %all-to-all-start = ((f32[4,32,16]{2,0,1:T(4,128)}), f32[4,32,16]{2,0,1:T(4,128)S(1)}, u32[]{:S(2)}, u32[]{:S(2)}) async-start(f32[4,32,16]{2,0,1:T(4,128)} %fusion.2), calls=%async_computation | async-start | bytes 131072 | tf_op jit(solution)/shard_map/all_to_all | solution.py:370
  82.0 10.0 %all-to-all-start.1 = ((f32[4,32,16]{2,0,1:T(4,128)}), f32[4,32,16]{2,0,1:T(4,128)S(1)}, u32[]{:S(2)}, u32[]{:S(2)}) async-start(f32[4,32,16]{2,0,1:T(4,128)} %copy.42), calls=%async_computation.1 | async-start | bytes 131072 | tf_op jit(solution)/shard_map/all_to_all | solution.py:375
where the time goes:
time: 94.6 us; the launch traced here: 94.2 us
  Pallas kernels  62.3 us (66%)
  waiting for transfers between devices  13.5 us (14%)
  local copies, waits for them, and re-layouts  8.8 us (9%)
  starting transfers between devices  5.14 us (5%)
  matrix products  2.82 us (3%)
    pallas_call x1, Pallas kernels, lattice(): pl.pallas_call(functools.partial(lattice_kernel, n_slab, n_md), out_shape...  46.4 us
    pallas_call x1, Pallas kernels, particles(): pl.pallas_call(particle_kernel, out_shape=(jax.ShapeDtypeStruct(pos.shape...  15.9 us
    all_to_all x1, waiting for transfers between devices, on_device(): lax.all_to_all(moms.reshape(4, devices, cap), ('slab', 'md'), split_axis=...  7.09 us
    all_to_all x1, waiting for transfers between devices, on_device(): lax.all_to_all(outgoing.reshape(4, devices, cap), ('slab', 'md'), split_a...  6.4 us
    unnamed x11, local copies, waits for them, and re-layouts  4.95 us
    all_to_all x1, starting transfers between devices, on_device(): lax.all_to_all(moms.reshape(4, devices, cap), ('slab', 'md'), split_axis=...  2.57 us
    all_to_all x1, starting transfers between devices, on_device(): lax.all_to_all(outgoing.reshape(4, devices, cap), ('slab', 'md'), split_a...  2.57 us
    dot_general x1, matrix products, on_device(): jnp.dot(vals, placed, precision=highest, preferred_element_type=jnp.float32)  2.42 us
  transfers between devices with their start and end apart: 2, of which 2 were waited for; matrix products, arithmetic and copies ran while one was open for 1% of the time, Pallas kernels for 0%

commit v1 on v0

v1 whole, which is shorter than its diff:
```python
import functools

import jax
import jax.numpy as jnp
from jax import lax
from jax.experimental import pallas as pl
from jax.experimental.pallas import tpu as pltpu
from jax.sharding import PartitionSpec as P

LB_STEPS = 4
MD_STEPS = 5

ORDER = [13, 1, 7, 9, 11, 5, 15, 18, 14, 2, 8, 10, 12, 6, 16, 17, 0, 3, 4]
lattice_dirs = [
    (0, 0, 0),
    (1, 0, 0),
    (-1, 0, 0),
    (0, 1, 0),
    (0, -1, 0),
    (0, 0, 1),
    (0, 0, -1),
    (1, 1, 0),
    (-1, -1, 0),
    (1, -1, 0),
    (-1, 1, 0),
    (1, 0, 1),
    (-1, 0, -1),
    (1, 0, -1),
    (-1, 0, 1),
    (0, 1, 1),
    (0, -1, -1),
    (0, 1, -1),
    (0, -1, 1),
]
DIRS = [lattice_dirs[i] for i in ORDER]
velocity_scale = 10.0
pair_strength = 0.5
friction = 2.0
time_step = 0.1
MESH = pl.DeviceIdType.MESH


def total_of(terms):
    terms = list(terms)
    while len(terms) > 1:
        terms = [a + b for a, b in zip(terms[::2], terms[1::2])] + (
            [terms[-1]] if len(terms) % 2 else []
        )
    return terms[0]


def fields(f):
    density = total_of(f)
    inverse = 1.0 / density
    vel = []
    for axis in range(3):
        plus = total_of(f[p] for p in range(19) if DIRS[p][axis] == 1)
        minus = total_of(f[p] for p in range(19) if DIRS[p][axis] == -1)
        vel.append((plus - minus) * inverse)
    return density, vel


def collided(f, relax):
    density, (vx, vy, vz) = fields(f)
    base = 1.0 - 1.5 * (vx * vx + vy * vy + vz * vz)
    keep = 1.0 - relax
    scale = relax * density
    result = [None] * 19
    for p, c in enumerate(DIRS):
        if result[p] is not None:
            continue
        size = sum(abs(e) for e in c)
        if size == 0:
            result[p] = keep * f[p] + (scale * (1.0 / 3.0)) * base
            continue
        along = total_of(v if e == 1 else -v for e, v in zip(c, (vx, vy, vz)) if e)
        weight = scale * (1.0 / 18.0 if size == 1 else 1.0 / 36.0)
        even = weight * (base + 4.5 * (along * along))
        odd = weight * (3.0 * along)
        q = DIRS.index(tuple(-e for e in c))
        result[p] = keep * f[p] + (even + odd)
        result[q] = keep * f[q] + (even - odd)
    return result


def lane_gather(table, index):
    return jnp.take_along_axis(table, index, axis=1, mode="promise_in_bounds")


def thirds(value):
    parts = []
    for _ in range(3):
        piece = value.astype(jnp.bfloat16).astype(jnp.float32)
        parts.append(piece)
        value = value - piece
    return parts


def by_hits(data, hits, dims):
    return lax.dot_general(
        data.astype(jnp.bfloat16), hits, (dims, ((), ())), preferred_element_type=jnp.float32
    )


def coupled_kernel(
    n_slab,
    n_md,
    f_ref,
    relax_ref,
    own_ref,
    pos_ref,
    vel_ref,
    nbr_ref,
    slots_ref,
    out_ref,
    pos_out,
    vel_out,
    cell_out,
    post,
    rows_out,
    rows_in,
    mean_ref,
    at,
    pull,
    data,
    hits,
    placed,
    tgt,
    table,
    blocks_out,
    blocks_in,
    send,
    recv,
    swap_send,
    swap_recv,
):
    cz, cx, ny = relax_ref.shape
    top_z = cz - 1
    cells = cz * cx
    entries, atoms = nbr_ref.shape
    groups = atoms // 128
    slot_count = hits.shape[0]
    devices = n_slab * n_md
    cap = slot_count // devices
    slab, md = lax.axis_index("slab"), lax.axis_index("md")
    me = slab * n_md + md
    above, below = lax.rem(slab + 1, n_slab), lax.rem(slab + n_slab - 1, n_slab)
    right, left = lax.rem(md + 1, n_md), lax.rem(md + n_md - 1, n_md)
    barrier = pltpu.get_barrier_semaphore()

    def coords(device):
        return (lax.div(device, n_md), lax.rem(device, n_md))

    def greet(k, carry):
        peer = coords(lax.rem(me + k, devices))
        pl.semaphore_signal(barrier, inc=1, device_id=peer, device_id_type=MESH)
        return carry

    lax.fori_loop(1, devices, greet, 0)

    def load(step, z, x0):
        if step == 0:
            return [f_ref[ORDER[p], z, pl.ds(x0, 8), :] for p in range(19)]
        return [
            post[step - 1, p, z + 1 - c[2], pl.ds(x0 + (8 - c[0]), 8), :]
            for p, c in enumerate(DIRS)
        ]

    def plane(step, z):
        def block(b, carry):
            x0 = pl.multiple_of(b * 8, 8)
            done = collided(load(step, z, x0), relax_ref[z, pl.ds(x0, 8), :])
            for p, c in enumerate(DIRS):
                value = done[p] if c[1] == 0 else pltpu.roll(done[p], c[1] % ny, axis=1)
                post[step, p, z + 1, pl.ds(x0 + 8, 8), :] = value
            return carry

        lax.fori_loop(0, cx // 8, block, 0, unroll=2)
        for side, first, row in ((0, 0, 7 + cx), (1, 8, 8)):
            for j in range(5):
                rows_out[step, z, side, j, :] = post[step, first + j, z + 1, row, :]

    copies = []

    def copy(step, slot, src, dst, peer):
        made = pltpu.make_async_remote_copy(
            src_ref=src,
            dst_ref=dst,
            send_sem=send.at[step, slot],
            recv_sem=recv.at[step, slot],
            device_id=peer,
            device_id_type=MESH,
        )
        made.start()
        copies.append(made)
        return made

    own = pl.ds(8, cx)

    def send_rows(step, z):
        return [
            copy(
                step,
                7 + 2 * z + side,
                rows_out.at[step, z, side],
                rows_in.at[step, z + 1, side],
                (slab, (right, left)[side]),
            )
            for side in range(2)
        ]

    def send_z(step, rising):
        z, slot, peer = (top_z, 0, above) if rising else (0, cz + 1, below)
        base = 0 if rising else 3
        made = [
            copy(
                step,
                base + 1 + side,
                rows_out.at[step, z, side],
                rows_in.at[step, slot, side],
                (peer, (right, left)[side]),
            )
            for side in range(2)
        ]
        spans = ((4, 5, 0),) if rising else ((12, 4, 3), (0, 1, 6))
        for first, count, sem in spans:
            made.append(
                copy(
                    step,
                    sem,
                    post.at[step, pl.ds(first, count), z + 1, own, :],
                    post.at[step, pl.ds(first, count), slot, own, :],
                    (peer, md),
                )
            )
        return made

    def arrive(made):
        for one in made:
            one.wait_recv()

    def put_rows(step):
        for z in range(cz):
            for side, first, row in ((0, 0, 7), (1, 8, 8 + cx)):
                for j in range(5):
                    post[step, first + j, z + 1, row, :] = rows_in[step, z + 1, side, j, :]

    def put_corners(step, rising):
        slot = 0 if rising else cz + 1
        for side, row in ((0, 7), (1, 8 + cx)):
            j = (4, 0)[side] if rising else (0, 4)[side]
            post[step, 8 * side + j, slot, row, :] = rows_in[step, slot, side, j, :]

    def pair_forces():
        def one_group(g, inner):
            mine = [jnp.broadcast_to(at[c, pl.ds(g, 1), :], (8, 128)) for c in range(3)]
            sums = [jnp.zeros((8, 128), jnp.float32)] * 3
            for k in range(0, entries, 8):
                index = nbr_ref[pl.ds(k, 8), pl.ds(pl.multiple_of(g * 128, 128), 128)]
                lane, row = index & 127, index >> 7
                found = [None] * 3
                for h in range(groups):
                    pick = row == h
                    for c in range(3):
                        line = jnp.broadcast_to(at[c, pl.ds(h, 1), :], (8, 128))
                        value = lane_gather(line, lane)
                        found[c] = value if h == 0 else jnp.where(pick, value, found[c])
                gap = [found[c] - mine[c] for c in range(3)]
                weight = jnp.exp(-0.5 * (gap[0] * gap[0] + gap[1] * gap[1] + gap[2] * gap[2]))
                sums = [sums[c] + gap[c] * weight for c in range(3)]
            for c in range(3):
                pull[c, pl.ds(g, 1), :] = jnp.sum(sums[c], axis=0, keepdims=True)
            return inner

        lax.fori_loop(0, groups, one_group, 0)

    def prepare_particles():
        for g in range(groups):
            here = pl.ds(g * 128, 128)
            for c in range(3):
                at[c, pl.ds(g, 1), :] = pos_ref[pl.ds(c, 1), here]
                at[3 + c, pl.ds(g, 1), :] = vel_ref[pl.ds(c, 1), here]
        pair_forces()

    def prepare_hits():
        data[...] = jnp.ones(data.shape, jnp.float32)
        tgt[...] = jnp.zeros(tgt.shape, jnp.float32)
        table[...] = jnp.zeros(table.shape, jnp.float32)
        for g in range(groups):
            label = lax.broadcasted_iota(jnp.int32, (slot_count, 128), 0)
            same = label == slots_ref[pl.ds(g, 1), :]
            hits[:, pl.ds(g * 128, 128)] = jnp.where(same, 1.0, 0.0).astype(jnp.bfloat16)

    def prepare_routes():
        top = own_ref.shape[0]
        label = lax.broadcasted_iota(jnp.int32, (devices, cells), 0)
        owned = [jnp.where(label == own_ref[pl.ds(k, 1), :], 1.0, 0.0) for k in range(top)]
        earlier = lax.broadcasted_iota(jnp.int32, (cells, cells), 0) < lax.broadcasted_iota(
            jnp.int32, (cells, cells), 1
        )
        before = by_hits(
            total_of(owned), jnp.where(earlier, 1.0, 0.0).astype(jnp.bfloat16), ((1,), (0,))
        )
        start = (label * cap).astype(jnp.float32)
        place = lax.broadcasted_iota(jnp.int32, (slot_count, cells), 0).astype(jnp.float32)
        filled = jnp.zeros((slot_count, cells), jnp.float32)
        for k in range(top):
            spot = jnp.sum((before + start) * owned[k], axis=0, keepdims=True)
            filled = filled + jnp.where(place == spot, 1.0, 0.0)
            before = before + owned[k]
        placed[...] = filled.astype(jnp.bfloat16)

    def swap(turn, values):
        per = 128 // cap
        for d in range(devices):
            chunk = values[:, d // per * 128 : (d // per + 1) * 128]
            shift = (128 - d % per * cap) % 128
            blocks_out[turn, d] = chunk if shift == 0 else pltpu.roll(chunk, shift, axis=1)

        def trade(k):
            to = lax.rem(me + k, devices)
            return pltpu.make_async_remote_copy(
                src_ref=blocks_out.at[turn, to],
                dst_ref=blocks_in.at[turn, me],
                send_sem=swap_send.at[turn, k],
                recv_sem=swap_recv.at[turn, k],
                device_id=coords(to),
                device_id_type=MESH,
            )

        def begin(k, carry):
            trade(k).start()
            return carry

        def landed(k, carry):
            origin = lax.rem(me + devices - k, devices)
            pltpu.make_async_remote_copy(
                src_ref=blocks_out.at[turn, origin],
                dst_ref=blocks_in.at[turn, origin],
                send_sem=swap_send.at[turn, k],
                recv_sem=swap_recv.at[turn, k],
                device_id=coords(origin),
                device_id_type=MESH,
            ).wait_recv()
            return carry

        def sent(k, carry):
            trade(k).wait_send()
            return carry

        lax.fori_loop(1, devices, begin, 0)
        blocks_in[turn, me] = blocks_out[turn, me]
        lax.fori_loop(1, devices, landed, 0)
        zone = lax.broadcasted_iota(jnp.int32, (4, 128), 1) // cap
        lines = []
        for h in range(slot_count // 128):
            line = jnp.zeros((4, 128), jnp.float32)
            for j in range(per):
                value = blocks_in[turn, h * per + j]
                if j:
                    value = pltpu.roll(value, j * cap, axis=1)
                line = jnp.where(zone == j, value, line)
            lines.append(line)
        return lines, lambda: lax.fori_loop(1, devices, sent, 0)

    last = {}
    plane(0, 0)
    for z in range(1, top_z):
        plane(0, z)
    pl.semaphore_wait(barrier, devices - 1)
    rows = []
    for z in range(top_z):
        rows += send_rows(0, z)
    last[False] = send_z(0, False)
    plane(0, top_z)
    rows += send_rows(0, top_z)
    last[True] = send_z(0, True)
    prepare_particles()
    for step in range(1, LB_STEPS):
        arrive(rows)
        put_rows(step - 1)
        rows, coming = [], {}
        for rising in ((False, True), (True, False))[(step + 1) % 2]:
            arrive(last[rising])
            put_corners(step - 1, rising)
            levels = range(top_z) if rising else [top_z]
            for z in levels:
                plane(step, z)
                rows += send_rows(step, z)
            coming[not rising] = send_z(step, not rising)
        last = coming
        if step == 1:
            prepare_hits()
        if step == 2:
            prepare_routes()
    arrive(rows)
    put_rows(LB_STEPS - 1)
    for rising in ((False, True), (True, False))[(LB_STEPS + 1) % 2]:
        arrive(last[rising])
        put_corners(LB_STEPS - 1, rising)
        for z in range(top_z) if rising else [top_z]:

            def finish(b, carry, z=z):
                x0 = pl.multiple_of(b * 8, 8)
                f = load(LB_STEPS, z, x0)
                for p in range(19):
                    out_ref[ORDER[p], z, pl.ds(x0, 8), :] = f[p]
                density, vel = fields(f)
                for c, value in enumerate((*vel, density)):
                    mean_ref[c, pl.ds(x0 + z * cx, 8), :] = value
                return carry

            lax.fori_loop(0, cx // 8, finish, 0, unroll=2)
    for c in range(4):
        scale = (velocity_scale if c < 3 else 1.0) / ny
        mean = jnp.sum(mean_ref[c].T, axis=0, keepdims=True) * scale
        for part, piece in enumerate(thirds(mean)):
            tgt[pl.ds(part * 4 + c, 1), :] = piece
    sums = by_hits(tgt[...], placed[...], ((1,), (1,)))
    lines, sent_first = swap(0, sums[0:4] + sums[4:8] + sums[8:12])

    slots = slots_ref[...]
    lane, row = slots & 127, slots >> 7
    goal = []
    for c in range(4):
        value = jnp.zeros((groups, 128), jnp.float32)
        for h, line in enumerate(lines):
            spread = jnp.broadcast_to(line[c : c + 1, :], (groups, 128))
            value = jnp.where(row == h, lane_gather(spread, lane), value)
        goal.append(value)
    rate = friction * goal[3]

    def advance():
        for c in range(3):
            vel = at[3 + c]
            force = pair_strength * pull[c] + rate * (goal[c] - vel)
            vel = vel + time_step * force
            at[3 + c] = vel
            at[c] = at[c] + time_step * vel

    def one_step(step, carry):
        pair_forces()
        advance()
        return carry

    advance()
    lax.fori_loop(1, MD_STEPS, one_step, 0)
    at[6] = at[3] * at[3] + at[4] * at[4] + at[5] * at[5]
    for c in range(4):
        for part, piece in enumerate(thirds(at[3 + c])):
            for g in range(groups):
                data[pl.ds(part * 4 + c, 1), pl.ds(g * 128, 128)] = piece[g : g + 1, :]
    sums = by_hits(data[...], hits[...], ((1,), (1,)))
    moments = (sums[0:4] + sums[4:8] + sums[8:12]) / jnp.maximum(sums[12:13], 1.0)
    lines, sent_second = swap(1, moments)
    for h, line in enumerate(lines):
        for part, piece in enumerate(thirds(line)):
            table[pl.ds(part * 4, 4), pl.ds(h * 128, 128)] = piece
    sums = by_hits(table[...], placed[...], ((1,), (0,)))
    picked = sums[0:4] + sums[4:8] + sums[8:12]
    for c in range(4):
        for z in range(cz):
            cell_out[c, pl.ds(z, 1), :] = picked[c : c + 1, z * cx : (z + 1) * cx]
    for g in range(groups):
        here = pl.ds(g * 128, 128)
        for c in range(3):
            pos_out[pl.ds(c, 1), here] = at[c, pl.ds(g, 1), :]
            vel_out[pl.ds(c, 1), here] = at[3 + c, pl.ds(g, 1), :]
    sent_first()
    sent_second()
    for made in copies:
        made.wait_send()


def on_device(populations, relax, owners, positions, velocities, neighbours, atom_slots):
    cz, cx, ny = relax.shape
    n_slab = lax.axis_size("slab")
    n_md = lax.axis_size("md")
    devices = n_slab * n_md
    top = owners.shape[2]
    cap = cz * max(2, 2 * cx * top // devices)
    slots = devices * cap
    atoms, entries = neighbours.shape
    groups = atoms // 128
    cells = cz * cx
    vmem = pl.BlockSpec(memory_space=pltpu.VMEM)
    dma = pltpu.SemaphoreType.DMA
    return pl.pallas_call(
        functools.partial(coupled_kernel, n_slab, n_md),
        out_shape=(
            jax.ShapeDtypeStruct(populations.shape, jnp.float32),
            jax.ShapeDtypeStruct(positions.shape, jnp.float32),
            jax.ShapeDtypeStruct(velocities.shape, jnp.float32),
            jax.ShapeDtypeStruct((4, cz, cx), jnp.float32),
        ),
        in_specs=[vmem] * 7,
        out_specs=(vmem,) * 4,
        scratch_shapes=[
            pltpu.VMEM((LB_STEPS, 19, cz + 2, cx + 16, ny), jnp.float32),
            pltpu.VMEM((LB_STEPS, cz, 2, 8, ny), jnp.float32),
            pltpu.VMEM((LB_STEPS, cz + 2, 2, 8, ny), jnp.float32),
            pltpu.VMEM((4, cells, ny), jnp.float32),
            pltpu.VMEM((7, groups, 128), jnp.float32),
            pltpu.VMEM((3, groups, 128), jnp.float32),
            pltpu.VMEM((16, atoms), jnp.float32),
            pltpu.VMEM((slots, atoms), jnp.bfloat16),
            pltpu.VMEM((slots, cells), jnp.bfloat16),
            pltpu.VMEM((16, cells), jnp.float32),
            pltpu.VMEM((16, slots), jnp.float32),
            pltpu.VMEM((2, devices, 4, 128), jnp.float32),
            pltpu.VMEM((2, devices, 4, 128), jnp.float32),
            dma((LB_STEPS, 7 + 2 * cz)),
            dma((LB_STEPS, 7 + 2 * cz)),
            dma((2, devices)),
            dma((2, devices)),
        ],
        compiler_params=pltpu.CompilerParams(
            collective_id=0, has_side_effects=True, vmem_limit_bytes=40 * 1024 * 1024
        ),
        name="coupled",
    )(
        populations,
        relax,
        owners.reshape(cells, top).T,
        positions,
        velocities,
        neighbours.T,
        atom_slots.reshape(groups, 128),
    )


def solution(mesh):
    return jax.shard_map(
        on_device,
        mesh=mesh,
        in_specs=(
            P(None, "slab", "md", None),
            P("slab", "md", None),
            P("slab", "md", None),
            P(None, ("slab", "md")),
            P(None, ("slab", "md")),
            P(("slab", "md"), None),
            P(("slab", "md")),
        ),
        out_specs=(
            P(None, "slab", "md", None),
            P(None, ("slab", "md")),
            P(None, ("slab", "md")),
            P(None, "slab", "md"),
        ),
        check_vma=False,
    )
```

time: 94.6 us -> 80.9 us (0.86)
  waiting for transfers between devices: 13.5 us -> 0 us
  Pallas kernels: 62.3 us -> 71 us
  starting transfers between devices: 5.14 us -> 0 us
  matrix products: 2.82 us -> 0 us
    all_to_all x2 -> x0, waiting for transfers between devices: 13.5 us -> none  [the longest x1 7.09 us: on_device(): lax.all_to_all(moms.reshape(4, devices, cap), ('slab', 'md'), split_axis=...]
    pallas_call x2 -> x1, Pallas kernels: 62.3 us -> 71 us  [on_device(): pl.pallas_call(functools.partial(coupled_kernel, n_slab, n_md), out_shape...]
    all_to_all x2 -> x0, starting transfers between devices: 5.14 us -> none  [the longest x1 2.57 us: on_device(): lax.all_to_all(moms.reshape(4, devices, cap), ('slab', 'md'), split_axis=...]
    unnamed x11 -> x17, local copies, waits for them, and re-layouts: 4.95 us -> 8.72 us
    reshape x6 -> x1, local copies, waits for them, and re-layouts: 3.08 us -> 0.08 us  [on_device(): owners.reshape(cells, top)]
    dot_general x2 -> x0, matrix products: 2.82 us -> none  [the longest x1 2.42 us: on_device(): jnp.dot(vals, placed, precision=highest, preferred_element_type=jnp.float32)]
  transfers between devices with their start and end apart: 2 -> 0, of which waited for: 2 -> 0; matrix products, arithmetic and copies ran while one was open for 1% -> 0% of each run, Pallas kernels for 0% -> 0%
where the time goes in v1:
time: 80.9 us; the launch traced here: 80.5 us
  Pallas kernels  71 us (88%)
  local copies, waits for them, and re-layouts  8.81 us (11%)
    pallas_call x1, Pallas kernels, on_device(): pl.pallas_call(functools.partial(coupled_kernel, n_slab, n_md), out_shape...  71 us
    unnamed x17, local copies, waits for them, and re-layouts  8.72 us

profile of v1, /device:TPU:0, one launch (start us, length us, event | category | flops | bytes accessed | tf_op | source)
XLA Modules:
  0.0 80.5 jit_solution(10505898451155002427)
XLA Ops:
  0.6 0.7 copy.11
  1.3 0.1 reshape.14
  1.4 0.0 copy-start
  1.4 1.3 %copy-done = f32[19,2,64,128]{3,2,1,0:T(8,128)S(1)} copy-done((f32[19,2,64,128]{3,2,1,0:T(8,128)S(1)}, f32[19,2,64,128]{3,2,1,0:T(8,128)}, u32[]{:S(2)}) %copy-start) | copy-done | bytes 1245208
  2.7 0.0 copy-start.1
  2.7 0.9 %copy-done.1 = s32[1024,64]{0,1:T(8,128)S(1)} copy-done((s32[1024,64]{0,1:T(8,128)S(1)}, s32[1024,64]{0,1:T(8,128)}, u32[]{:S(2)}) %copy-start.1) | copy-done | bytes 262168
  3.6 0.0 copy-start.2
  3.6 0.8 %copy-done.2 = f32[2,64,128]{2,1,0:T(8,128)S(1)} copy-done((f32[2,64,128]{2,1,0:T(8,128)S(1)}, f32[2,64,128]{2,1,0:T(8,128)}, u32[]{:S(2)}) %copy-start.2) | copy-done | bytes 65560
  4.5 0.0 copy-start.3
  4.5 0.7 copy-done.3
  5.2 0.0 copy-start.4
  5.2 0.7 copy-done.4
  5.9 0.0 copy-start.5
  5.9 0.7 copy-done.5
  6.6 71.0 %coupled.1 = (f32[19,2,64,128]{3,2,1,0:T(8,128)S(1)}, f32[3,1024]{1,0:T(4,128)S(1)}, f32[3,1024]{1,0:T(4,128)S(1)}, f32[4,2,64]{2,1,0:T(2,128)S(1)}) custom-call(f32[19,2,64,128]{3,2,1,0:T(8,128)S(1)} %copy-done, f32[2,64,128]{2,1,0:T(8,128)S(1)} %copy-done.2, s32[2,128]{1,0:T(2,128)S(1)} %bitcast.7, f32[3,1024]{1,0:T(4,128)S(1)} %copy-done.3, ...), custom_call_target="tpu_custom_call" | custom-call | tf_op jit(solution)/shard_map/coupled/pallas_call | solution.py:488
  77.6 1.0 %copy.16 = f32[19,2,64,128]{3,2,1,0:T(8,128)} copy(f32[19,2,64,128]{3,2,1,0:T(8,128)S(1)} %get-tuple-element.8) | data formatting | bytes 2490368
  78.7 0.6 copy.17
  79.3 0.6 copy.18
  79.9 0.6 copy.19
Async XLA Ops:
  1.4 1.3 %copy-start = (f32[19,2,64,128]{3,2,1,0:T(8,128)S(1)}, f32[19,2,64,128]{3,2,1,0:T(8,128)}, u32[]{:S(2)}) copy-start(f32[19,2,64,128]{3,2,1,0:T(8,128)} %f_ref.1) | copy-start | bytes 3735556
  2.7 0.9 %copy-start.1 = (s32[1024,64]{0,1:T(8,128)S(1)}, s32[1024,64]{0,1:T(8,128)}, u32[]{:S(2)}) copy-start(s32[1024,64]{0,1:T(8,128)} %param.12) | copy-start | bytes 786436
  3.6 0.8 %copy-start.2 = (f32[2,64,128]{2,1,0:T(8,128)S(1)}, f32[2,64,128]{2,1,0:T(8,128)}, u32[]{:S(2)}) copy-start(f32[2,64,128]{2,1,0:T(8,128)} %relax_ref.1) | copy-start | bytes 196612
  4.5 0.7 copy-start.3
  5.2 0.7 copy-start.4
  5.9 0.7 copy-start.5
